TPU v7x, 32 devices: a whole 2x2x4 slice. The times are simulated.
32 devices in a mesh: tm: 8 (over z, y), mp: 4 (over x, core).
Axes of the slice: x: 2, y: 2, z: 4, core: 2. Of those that a mesh axis runs over, the one named last changes fastest.
Arguments:
- latents: float32 [4, 8, 4, 4096], P(None, 'tm'), may hold values from -6 to 6
- noise: float32 [4, 8, 4, 4096], P(None, 'tm'), may hold values from -6 to 6
- start_step: int32 [4], replicated, may hold values from 8 to 999
- slide: int32 [4], replicated, may hold values from 1 to 8, as said below
- w_in: float32 [4, 320], replicated, may hold values from -3 to 3
- w_gate: bfloat16 [320, 1280], P(None, 'mp'), may hold values from -0.3125 to 0.3125
- w_value: bfloat16 [320, 1280], P(None, 'mp'), may hold values from -0.3125 to 0.3125
- w_down: bfloat16 [1280, 320], P('mp'), may hold values from -0.15625 to 0.15625
- w_out: float32 [320, 4], replicated, may hold values from -0.3125 to 0.3125
Outputs:
- next_window: float32 [4, 8, 4, 4096], P(None, 'tm')
- eps: float32 [4, 8, 4, 4096], P(None, 'tm', None, 'mp')
Inputs may be any that keep to these rules, and one draw needn't show every extreme that they name: `slide`: some prompt slides by exactly 8, and another by exactly 1.
All inputs are finite; a program needn't handle non-finite values.
Results may differ from a plain program's by a relative error of at most 0.0023.
Values sent between devices are 32-bit elements; how exact they have to be, the bound alone decides.
No kernel may reach another device: no remote copies, remote signals or barrier semaphores. Data moves between devices by JAX's collectives and lax.ppermute only.
A program may use at most 64 MiB of HBM per device.

v0:
```python
import math
import jax
import jax.numpy as jnp
from jax import lax
from jax.sharding import PartitionSpec as P

TSTEPS = 1000


def prefix(x, axis, combine, identity):
    peers, mine = (lax.axis_size(axis), lax.axis_index(axis))
    everything = lax.all_gather(x, axis)
    start = jnp.broadcast_to(jnp.asarray(identity, x.dtype), x.shape)

    def lap(k, before):
        reached = k < mine
        new = combine(before, everything[k])
        return jnp.where(reached, new, before)

    return lax.fori_loop(0, peers, lap, start)


def from_root(block, axis, holder):
    block = jnp.where(lax.axis_index(axis) == holder, block, jnp.zeros_like(block))
    return lax.psum(block, axis)


def from_behind(block, axis, distance):
    devices = range(lax.axis_size(axis))
    route = [(i - distance, i) for i in devices if i - distance in devices]
    return lax.ppermute(block, axis, route)


def plan(count):
    steps_f = jnp.arange(count, dtype=jnp.float32)
    beta = 0.0001 + (0.02 - 0.0001) * steps_f / (count - 1)
    abar = jnp.cumprod(1.0 - beta)
    return (beta, abar)


def lookup(table, times):
    grid = jnp.arange(table.shape[0], dtype=jnp.int32)
    return jnp.sum(jnp.where(times[..., None] == grid, table, 0.0), axis=-1)


def embed(times, channels):
    half = channels // 2
    freq = jnp.exp(-math.log(10000.0) * jnp.arange(half, dtype=jnp.float32) / half)
    angle = times[..., None] * freq
    return jnp.concatenate([jnp.cos(angle), jnp.sin(angle)], axis=-1)


def add_terms(earlier, later):
    return earlier + later


def shards(latents, noise, start_step, slide, w_in, w_gate, w_value, w_down, w_out):
    prompts, t_dev, lat, pos = latents.shape
    channels = w_in.shape[1]
    n_tm = lax.axis_size("tm")
    window = n_tm * t_dev
    share_width = pos // lax.axis_size("mp")
    share_offset = lax.axis_index("mp") * share_width
    slots = lax.axis_index("tm") * t_dev + jnp.arange(t_dev, dtype=jnp.int32)
    times = start_step[:, None] - slots[None, :]
    beta, abar = plan(TSTEPS)
    beta_t = lookup(beta, times)[:, :, None, None]
    abar_t = lookup(abar, times)[:, :, None, None]
    vectors = embed(times.astype(jnp.float32), channels).reshape(prompts * t_dev, channels)
    folded = jnp.dot(w_down.astype(jnp.float32), w_out, precision=lax.Precision.HIGHEST)
    items = latents.reshape(prompts * t_dev, lat, pos)

    def denoise(pair):
        latent, vector = pair
        hid = jnp.dot(w_in.T, latent, precision=lax.Precision.HIGHEST) + vector[:, None]
        mean = jnp.mean(hid, axis=0)
        var = jnp.mean((hid - mean) ** 2, axis=0)
        normed = ((hid - mean) * lax.rsqrt(var + 1e-05)).astype(jnp.bfloat16)
        gate = jnp.einsum("cf,cp->fp", w_gate, normed, preferred_element_type=jnp.float32)
        value = jnp.einsum("cf,cp->fp", w_value, normed, preferred_element_type=jnp.float32)
        hidden = (jax.nn.gelu(gate, approximate=False) * value).astype(jnp.bfloat16)
        partial_eps = jnp.dot(folded.T, hidden, precision=lax.Precision.HIGHEST)
        base_eps = jnp.dot(w_out.T, hid, precision=lax.Precision.HIGHEST)
        return (partial_eps, base_eps)

    partials, bases = lax.map(denoise, (items, vectors))
    eps = lax.psum(partials, "mp") + bases
    eps = eps.reshape(prompts, t_dev, lat, pos)
    eps_share = lax.dynamic_slice_in_dim(eps, share_offset, share_width, 3)
    stepped = (latents - beta_t / jnp.sqrt(1.0 - abar_t) * eps) / jnp.sqrt(1.0 - beta_t) + jnp.sqrt(
        beta_t
    ) * noise
    drift = stepped - latents
    first = (slots == 0)[None, :, None, None]
    head_part = jnp.where(first, latents, 0.0)
    terms = drift + head_part
    totals = jnp.sum(terms, axis=1)
    before = prefix(totals, "tm", add_terms, jnp.zeros_like(totals))
    updated = before[:, None] + (jnp.cumsum(terms, axis=1) - terms) + head_part
    last = from_root(updated[:, -1], "tm", n_tm - 1)
    moved = updated
    for bit in range((window // 2).bit_length()):
        step = 1 << bit
        incoming = from_behind(moved, "tm", -max(1, step // t_dev))
        taken = slide >> bit & 1 == 1
        moved = jnp.where(taken[:, None, None, None], incoming, moved)
    beyond = slots[None, :] + slide[:, None] >= window
    result = jnp.where(beyond[:, :, None, None], last[:, None], moved)
    return (result, eps_share)


def solution(mesh):
    in_specs = (
        P(None, "tm", None, None),
        P(None, "tm", None, None),
        P(),
        P(),
        P(),
        P(None, "mp"),
        P(None, "mp"),
        P("mp", None),
        P(),
    )
    out_specs = (P(None, "tm", None, None), P(None, "tm", None, "mp"))
    return jax.shard_map(shards, mesh=mesh, in_specs=in_specs, out_specs=out_specs, check_vma=False)
```

profile of v0, /device:TPU:0, one launch (start us, length us, event | category | flops | bytes accessed | tf_op | source)
XLA Modules:
  0.0 305.6 jit_solution(13553774158699933047)
XLA Ops:
  7.3 1.2 fusion.29
  8.6 1.0 fusion.31
  9.6 99.3 %while.26 = (s32[]{:T(128)}, f32[4,4,4096]{2,1,0:T(4,128)S(1)}, f32[4,4,4096]{2,1,0:T(4,128)S(1)}, f32[4,4,4096]{2,1,0:T(4,128)}, f32[4,320]{1,0:T(4,128)}, /*in...) while((s32[]{:T(128)}, f32[4,4,4096]{2,1,0:T(4,128)S(1)}, ...), condition=%wide.region_7.8_spmd, body=%wide.region_4.7_spmd.sunk | while | flops 1967394816 | bytes 44411340 | solution.py:86
  9.7 5.4 %fusion.60 = (f32[4096]{0:T(1024)S(1)}, f32[4096,320]{0,1:T(8,128)S(1)}) fusion(f32[320]{0:T(512)S(1)} %dynamic-slice_reduce_fusion.2, f32[4,320]{1,0:T(4,128)} %get-tuple-element.315, f32[4,4,4096]{2,1,0:T(4,128)} %get-tuple-element.314, s32[]{:T(128)} %get-tuple-element.300), kind=kOutput, calls=%fused_computation.72.clone.1 | convolution fusion | flops 65531904 | bytes 5332736 | tf_op jit(solution)/shard_map/while/body/eval_jaxpr/dot_general | solution.py:75
  15.1 0.6 multiply_reduce_fusion.2
  15.7 1.6 fusion.61
  17.3 13.1 %fusion.62 = bf16[320,4096]{1,0:T(8,128)(2,1)S(1)} fusion(bf16[320,320]{1,0:T(8,128)(2,1)S(1)} %copy-done.8, f32[4096,320]{0,1:T(8,128)S(1)} %fusion.61, f32[4096,320]{0,1:T(8,128)S(1)} %get-tuple-element.283, f32[4096]{0:T(1024)S(1)} %add_rsqrt_fusion.2, f32[4096]{0:T(1024)S(1)} %broadcast_multiply_fusion.2), kind=kOutput, calls=%fused_computation.5.clone.1 | convolution fusion | flops 929300480 | bytes 13344768 | tf_op jit(solution)/shard_map/while/body/eval_jaxpr/cf,cp->fp/dot_general | solution.py:80
  30.5 1.1 fusion.63
  31.6 2.8 fusion.64
  34.5 5.3 %fusion.60 = (f32[4096]{0:T(1024)S(1)}, f32[4096,320]{0,1:T(8,128)S(1)}) fusion(f32[320]{0:T(512)S(1)} %dynamic-slice_reduce_fusion.2, f32[4,320]{1,0:T(4,128)} %get-tuple-element.315, f32[4,4,4096]{2,1,0:T(4,128)} %get-tuple-element.314, s32[]{:T(128)} %get-tuple-element.300), kind=kOutput, calls=%fused_computation.72.clone.1 | convolution fusion | flops 65531904 | bytes 5332736 | tf_op jit(solution)/shard_map/while/body/eval_jaxpr/dot_general | solution.py:75
  39.9 0.6 multiply_reduce_fusion.2
  40.5 1.6 fusion.61
  42.2 13.1 %fusion.62 = bf16[320,4096]{1,0:T(8,128)(2,1)S(1)} fusion(bf16[320,320]{1,0:T(8,128)(2,1)S(1)} %copy-done.8, f32[4096,320]{0,1:T(8,128)S(1)} %fusion.61, f32[4096,320]{0,1:T(8,128)S(1)} %get-tuple-element.283, f32[4096]{0:T(1024)S(1)} %add_rsqrt_fusion.2, f32[4096]{0:T(1024)S(1)} %broadcast_multiply_fusion.2), kind=kOutput, calls=%fused_computation.5.clone.1 | convolution fusion | flops 929300480 | bytes 13344768 | tf_op jit(solution)/shard_map/while/body/eval_jaxpr/cf,cp->fp/dot_general | solution.py:80
  55.3 1.1 fusion.63
  56.5 2.8 fusion.64
  59.3 5.3 %fusion.60 = (f32[4096]{0:T(1024)S(1)}, f32[4096,320]{0,1:T(8,128)S(1)}) fusion(f32[320]{0:T(512)S(1)} %dynamic-slice_reduce_fusion.2, f32[4,320]{1,0:T(4,128)} %get-tuple-element.315, f32[4,4,4096]{2,1,0:T(4,128)} %get-tuple-element.314, s32[]{:T(128)} %get-tuple-element.300), kind=kOutput, calls=%fused_computation.72.clone.1 | convolution fusion | flops 65531904 | bytes 5332736 | tf_op jit(solution)/shard_map/while/body/eval_jaxpr/dot_general | solution.py:75
  64.7 0.6 multiply_reduce_fusion.2
  65.3 1.6 fusion.61
  67.0 13.1 %fusion.62 = bf16[320,4096]{1,0:T(8,128)(2,1)S(1)} fusion(bf16[320,320]{1,0:T(8,128)(2,1)S(1)} %copy-done.8, f32[4096,320]{0,1:T(8,128)S(1)} %fusion.61, f32[4096,320]{0,1:T(8,128)S(1)} %get-tuple-element.283, f32[4096]{0:T(1024)S(1)} %add_rsqrt_fusion.2, f32[4096]{0:T(1024)S(1)} %broadcast_multiply_fusion.2), kind=kOutput, calls=%fused_computation.5.clone.1 | convolution fusion | flops 929300480 | bytes 13344768 | tf_op jit(solution)/shard_map/while/body/eval_jaxpr/cf,cp->fp/dot_general | solution.py:80
  80.1 1.1 fusion.63
  81.3 2.8 fusion.64
  84.1 5.3 %fusion.60 = (f32[4096]{0:T(1024)S(1)}, f32[4096,320]{0,1:T(8,128)S(1)}) fusion(f32[320]{0:T(512)S(1)} %dynamic-slice_reduce_fusion.2, f32[4,320]{1,0:T(4,128)} %get-tuple-element.315, f32[4,4,4096]{2,1,0:T(4,128)} %get-tuple-element.314, s32[]{:T(128)} %get-tuple-element.300), kind=kOutput, calls=%fused_computation.72.clone.1 | convolution fusion | flops 65531904 | bytes 5332736 | tf_op jit(solution)/shard_map/while/body/eval_jaxpr/dot_general | solution.py:75
  90.1 1.6 fusion.61
  91.8 13.1 %fusion.62 = bf16[320,4096]{1,0:T(8,128)(2,1)S(1)} fusion(bf16[320,320]{1,0:T(8,128)(2,1)S(1)} %copy-done.8, f32[4096,320]{0,1:T(8,128)S(1)} %fusion.61, f32[4096,320]{0,1:T(8,128)S(1)} %get-tuple-element.283, f32[4096]{0:T(1024)S(1)} %add_rsqrt_fusion.2, f32[4096]{0:T(1024)S(1)} %broadcast_multiply_fusion.2), kind=kOutput, calls=%fused_computation.5.clone.1 | convolution fusion | flops 929300480 | bytes 13344768 | tf_op jit(solution)/shard_map/while/body/eval_jaxpr/cf,cp->fp/dot_general | solution.py:80
  104.9 1.1 fusion.63
  106.1 2.8 fusion.64
  108.9 0.7 copy-done.3
  110.5 34.3 %all-reduce.4.cloned.1.call-done = f32[4,4,4096]{2,1,0:T(4,128)} async-done(((f32[4,4,4096]{2,1,0:T(4,128)}), f32[4,4,4096]{2,1,0:T(4,128)}) %all-reduce.4.cloned.1.call-update) | async-done | bytes 262160 | tf_op jit(solution)/shard_map/psum | solution.py:87
  144.8 1.9 fusion.26
  146.8 49.8 %all-gather.3.cloned.1.call-done = f32[32,1,4,4096]{3,2,1,0:T(4,128)} async-done(((f32[4,1,4,4096]{3,2,1,0:T(4,128)}), f32[32,1,4,4096]{3,2,1,0:T(4,128)}) %all-gather.3.cloned.1.call-update) | async-done | bytes 2097168 | tf_op jit(solution)/shard_map/all_gather | solution.py:12
  196.6 10.1 %while.27 = (s32[]{:T(128)}, f32[4,4,4096]{2,1,0:T(4,128)S(1)}, s32[]{:T(128)}, f32[8,4,4,4096]{3,2,1,0:T(4,128)}, s32[]{:T(128)}, /*index=5*/s32[]{:T(128)}) while((s32[]{:T(128)}, f32[4,4,4096]{2,1,0:T(4,128)S(1)}, s32[]{:T(128)}, f32[8,4,4,4096]{3,2,1,0:T(4,128)}, s32[]{:T(128)}, /*index=5*/s32[]{:T(128)}) %tuple.75), condition=%wide.region_10.11_spmd.clone, body=%wide.region_9.10_spmd.clone.sunk | while | flops 196612 | bytes 786525 | solution.py:20
  196.6 1.2 add_select_fusion.2
  197.9 1.2 add_select_fusion.2
  199.1 1.2 add_select_fusion.2
  200.4 1.2 add_select_fusion.2
  201.6 1.2 add_select_fusion.2
  202.9 1.2 add_select_fusion.2
  204.2 1.2 add_select_fusion.2
  205.4 1.2 add_select_fusion.2
  206.7 1.8 broadcast_select_fusion
  208.5 1.3 collective-permute-start
  209.8 6.9 %collective-permute-done = f32[4,1,4,4096]{3,2,1,0:T(4,128)S(1)} collective-permute-done((f32[4,1,4,4096]{3,2,1,0:T(4,128)S(1)}, f32[4,1,4,4096]{3,2,1,0:T(4,128)S(1)}, u32[]{:S(2)}, u32[]{:S(2)}) %collective-permute-start) | collective-permute-done | bytes 262176 | tf_op jit(solution)/shard_map/ppermute | solution.py:31
  216.9 1.3 collective-permute-start.1
  218.2 7.1 %collective-permute-done.1 = f32[4,1,4,4096]{3,2,1,0:T(4,128)S(1)} collective-permute-done((f32[4,1,4,4096]{3,2,1,0:T(4,128)S(1)}, f32[4,1,4,4096]{3,2,1,0:T(4,128)S(1)}, u32[]{:S(2)}, u32[]{:S(2)}) %collective-permute-start.1) | collective-permute-done | bytes 262176 | tf_op jit(solution)/shard_map/ppermute | solution.py:31
  225.4 1.3 collective-permute-start.2
  226.7 0.6 dynamic-slice_bitcast_fusion
  227.4 69.9 %all-reduce.6.cloned.1.call-done = f32[4,1,4,4096]{3,2,1,0:T(4,128)} async-done(((f32[4,1,4,4096]{3,2,1,0:T(4,128)}), f32[4,1,4,4096]{3,2,1,0:T(4,128)}) %all-reduce.6.cloned.1.call-update) | async-done | bytes 262160 | tf_op jit(solution)/shard_map/psum | solution.py:25
  297.2 1.8 select_select_fusion
  (74 shorter events, 2.3 us)
Async XLA Ops:
  7.2 1.5 copy-start
  7.2 137.6 %all-reduce.4.cloned.1.call-start = ((), (), s32[]{:S(2)}) async-start(), calls=%async_computation | async-start | bytes 524288 | tf_op jit(solution)/shard_map/psum | solution.py:87
  9.6 100.7 %copy-start.6 = (s32[4]{0:T(128)S(1)}, s32[4]{0:T(128)}, u32[]{:S(2)}) copy-start(s32[4]{0:T(128)} %get-tuple-element.187) | copy-start | bytes 52
  9.6 135.2 %copy-start.4 = (f32[4,1,4,4096]{3,2,1,0:T(4,128)S(1)}, f32[4,1,4,4096]{3,2,1,0:T(4,128)}, u32[]{:S(2)}) copy-start(f32[4,1,4,4096]{3,2,1,0:T(4,128)} %param.14) | copy-start | bytes 786436
  9.7 6.0 %copy-start.1 = (bf16[320,320]{1,0:T(8,128)(2,1)S(1)}, bf16[320,320]{1,0:T(8,128)(2,1)}, u32[]{:S(2)}) copy-start(bf16[320,320]{1,0:T(8,128)(2,1)} %get-tuple-element.317) | copy-start | bytes 614404 | tf_op jit(solution)/shard_map/while
  15.7 1.6 copy-start.8
  17.3 14.3 %copy-start.5 = (f32[320,4]{0,1:T(4,128)S(1)}, f32[320,4]{0,1:T(4,128)}, u32[]{:S(2)}) copy-start(f32[320,4]{0,1:T(4,128)} %get-tuple-element.320) | copy-start | bytes 15364 | tf_op jit(solution)/shard_map/while
  34.5 6.0 %copy-start.1 = (bf16[320,320]{1,0:T(8,128)(2,1)S(1)}, bf16[320,320]{1,0:T(8,128)(2,1)}, u32[]{:S(2)}) copy-start(bf16[320,320]{1,0:T(8,128)(2,1)} %get-tuple-element.317) | copy-start | bytes 614404 | tf_op jit(solution)/shard_map/while
  40.5 1.6 copy-start.8
  42.1 14.3 %copy-start.5 = (f32[320,4]{0,1:T(4,128)S(1)}, f32[320,4]{0,1:T(4,128)}, u32[]{:S(2)}) copy-start(f32[320,4]{0,1:T(4,128)} %get-tuple-element.320) | copy-start | bytes 15364 | tf_op jit(solution)/shard_map/while
  59.3 6.0 %copy-start.1 = (bf16[320,320]{1,0:T(8,128)(2,1)S(1)}, bf16[320,320]{1,0:T(8,128)(2,1)}, u32[]{:S(2)}) copy-start(bf16[320,320]{1,0:T(8,128)(2,1)} %get-tuple-element.317) | copy-start | bytes 614404 | tf_op jit(solution)/shard_map/while
  65.3 1.6 copy-start.8
  67.0 14.3 %copy-start.5 = (f32[320,4]{0,1:T(4,128)S(1)}, f32[320,4]{0,1:T(4,128)}, u32[]{:S(2)}) copy-start(f32[320,4]{0,1:T(4,128)} %get-tuple-element.320) | copy-start | bytes 15364 | tf_op jit(solution)/shard_map/while
  84.1 6.0 %copy-start.1 = (bf16[320,320]{1,0:T(8,128)(2,1)S(1)}, bf16[320,320]{1,0:T(8,128)(2,1)}, u32[]{:S(2)}) copy-start(bf16[320,320]{1,0:T(8,128)(2,1)} %get-tuple-element.317) | copy-start | bytes 614404 | tf_op jit(solution)/shard_map/while
  90.1 1.6 copy-start.8
  91.8 14.3 %copy-start.5 = (f32[320,4]{0,1:T(4,128)S(1)}, f32[320,4]{0,1:T(4,128)}, u32[]{:S(2)}) copy-start(f32[320,4]{0,1:T(4,128)} %get-tuple-element.320) | copy-start | bytes 15364 | tf_op jit(solution)/shard_map/while
  108.9 0.7 copy-start.3
  108.9 97.8 %copy-start.2 = (f32[4,4,4096]{2,1,0:T(4,128)S(1)}, f32[4,4,4096]{2,1,0:T(4,128)}, u32[]{:S(2)}) copy-start(f32[4,4,4096]{2,1,0:T(4,128)} %get-tuple-element.343) | copy-start | bytes 786436
  108.9 100.8 %copy-start.7 = (s32[4]{0:T(128)S(1)}, s32[4]{0:T(128)}, u32[]{:S(2)}) copy-start(s32[4]{0:T(128)} %param.16) | copy-start | bytes 52
  109.6 87.0 %all-gather.3.cloned.1.call-start = ((), (), s32[]{:S(2)}) async-start(), calls=%async_computation.2 | async-start | bytes 2359296 | tf_op jit(solution)/shard_map/all_gather | solution.py:12
  146.8 150.5 %all-reduce.6.cloned.1.call-start = ((), (), s32[]{:S(2)}) async-start(), calls=%async_computation.1 | async-start | bytes 524288 | tf_op jit(solution)/shard_map/psum | solution.py:25
  208.5 8.3 %collective-permute-start = (f32[4,1,4,4096]{3,2,1,0:T(4,128)S(1)}, f32[4,1,4,4096]{3,2,1,0:T(4,128)S(1)}, u32[]{:S(2)}, u32[]{:S(2)}) collective-permute-start(f32[4,1,4,4096]{3,2,1,0:T(4,128)S(1)} %get-tuple-element.183), channel_id=1, source_target_pairs={{4,0},{8,4},{12,8},{16,12},{20,16},{24,20},{28,24},{5,1},{9,5},{13... | collective-permute-start | bytes 786440 | tf_op jit(solution)/shard_map/ppermute | solution.py:31
  216.9 8.4 %collective-permute-start.1 = (f32[4,1,4,4096]{3,2,1,0:T(4,128)S(1)}, f32[4,1,4,4096]{3,2,1,0:T(4,128)S(1)}, u32[]{:S(2)}, u32[]{:S(2)}) collective-permute-start(f32[4,1,4,4096]{3,2,1,0:T(4,128)S(1)} %broadcast_select_fusion.1), channel_id=1, source_target_pairs={{8,0},{12,4},{16,8},{20,12},{24,16},{28,20},{9,1},{13,5},{17,9},{2... | collective-permute-start | bytes 786440 | tf_op jit(solution)/shard_map/ppermute | solution.py:31
  225.4 71.8 %collective-permute-start.2 = (f32[4,1,4,4096]{3,2,1,0:T(4,128)S(1)}, f32[4,1,4,4096]{3,2,1,0:T(4,128)S(1)}, u32[]{:S(2)}, u32[]{:S(2)}) collective-permute-start(f32[4,1,4,4096]{3,2,1,0:T(4,128)S(1)} %broadcast_select_fusion.2), channel_id=1, source_target_pairs={{16,0},{20,4},{24,8},{28,12},{17,1},{21,5},{25,9},{29,13},{18,2},{... | collective-permute-start | bytes 786440 | tf_op jit(solution)/shard_map/ppermute | solution.py:31
Sparse Core Ops, SparseCore 0:
  109.8 34.9 all-reduce.3
  147.5 49.0 all-gather.2
  218.3 78.8 all-reduce.5
where the time goes:
time: 306 us
  waiting for transfers between devices  168 us (55%)
  matrix products  97.2 us (32%)
  other arithmetic  20.2 us (7%)
  between operations  13.9 us (5%)
  starting transfers between devices  3.99 us (1%)
    psum x1, waiting for transfers between devices, from_root(): return lax.psum(block, axis)  69.9 us
    dot_general x4, matrix products, denoise(): jnp.einsum('cf,cp->fp', w_value, normed, preferred_element_type=jnp.float32)  52.5 us
    all_gather x1, waiting for transfers between devices, prefix(): everything = lax.all_gather(x, axis)  49.8 us
    psum x1, waiting for transfers between devices, shards(): eps = lax.psum(partials, 'mp') + bases  34.3 us
    dot_general x4, matrix products, denoise(): jnp.dot(w_in.T, latent, precision=lax.Precision.HIGHEST) + vector[:, None]  21.4 us
    ppermute x3, waiting for transfers between devices, from_behind(): return lax.ppermute(block, axis, route)  14 us
    dot_general x4, matrix products, denoise(): base_eps = jnp.dot(w_out.T, hid, precision=lax.Precision.HIGHEST)  11.3 us
    select_n x8, other arithmetic, lap(): return jnp.where(reached, new, before)  9.92 us
  transfers between devices with their start and end apart: 6, of which 5 were waited for; matrix products, arithmetic and copies ran while one was open for 1% of the time, Pallas kernels for 0%

commit v1 on v0

--- a/solution.py
+++ b/solution.py
@@ -84,7 +84,7 @@
         return (partial_eps, base_eps)
 
     partials, bases = lax.map(denoise, (items, vectors))
-    eps = lax.psum(partials, "mp") + bases
+    eps = jnp.sum(lax.all_gather(partials, "mp"), axis=0) + bases
     eps = eps.reshape(prompts, t_dev, lat, pos)
     eps_share = lax.dynamic_slice_in_dim(eps, share_offset, share_width, 3)
     stepped = (latents - beta_t / jnp.sqrt(1.0 - abar_t) * eps) / jnp.sqrt(1.0 - beta_t) + jnp.sqrt(

time: 306 us -> 292 us (0.954)
  waiting for transfers between devices: 168 us -> 152 us
    psum x1 -> x0, waiting for transfers between devices: 34.3 us -> none  [shards(): eps = lax.psum(partials, 'mp') + bases]
    all_gather x0 -> x1, waiting for transfers between devices: none -> 18.7 us  [shards(): eps = jnp.sum(lax.all_gather(partials, 'mp'), axis=0) + bases]
where the time goes in v1:
time: 292 us; the launch traced here: 291 us
  waiting for transfers between devices  152 us (52%)
  matrix products  97.2 us (33%)
  other arithmetic  21.6 us (7%)
  between operations  13.9 us (5%)
  starting transfers between devices  3.99 us (1%)
    psum x1, waiting for transfers between devices, from_root(): return lax.psum(block, axis)  69.9 us
    dot_general x4, matrix products, denoise(): jnp.einsum('cf,cp->fp', w_value, normed, preferred_element_type=jnp.float32)  52.5 us
    all_gather x1, waiting for transfers between devices, prefix(): everything = lax.all_gather(x, axis)  49.2 us
    dot_general x4, matrix products, denoise(): jnp.dot(w_in.T, latent, precision=lax.Precision.HIGHEST) + vector[:, None]  21.4 us
    all_gather x1, waiting for transfers between devices, shards(): eps = jnp.sum(lax.all_gather(partials, 'mp'), axis=0) + bases  18.7 us
    ppermute x3, waiting for transfers between devices, from_behind(): return lax.ppermute(block, axis, route)  14 us
    dot_general x4, matrix products, denoise(): base_eps = jnp.dot(w_out.T, hid, precision=lax.Precision.HIGHEST)  11.3 us
    select_n x8, other arithmetic, lap(): return jnp.where(reached, new, before)  9.92 us
  transfers between devices with their start and end apart: 6, of which 5 were waited for; matrix products, arithmetic and copies ran while one was open for 1% of the time, Pallas kernels for 0%

profile of v1, /device:TPU:0, one launch (start us, length us, event | category | flops | bytes accessed | tf_op | source)
XLA Modules:
  0.0 290.9 jit_solution(6478198163352663730)
XLA Ops:
  7.3 1.2 fusion.29
  8.7 1.0 fusion.31
  9.7 99.3 %while.26 = (s32[]{:T(128)}, f32[4,4,4096]{2,1,0:T(4,128)S(1)}, f32[4,4,4096]{2,1,0:T(4,128)S(1)}, f32[4,4,4096]{2,1,0:T(4,128)}, f32[4,320]{1,0:T(4,128)}, /*in...) while((s32[]{:T(128)}, f32[4,4,4096]{2,1,0:T(4,128)S(1)}, ...), condition=%wide.region_7.8_spmd, body=%wide.region_4.7_spmd.sunk | while | flops 1967394816 | bytes 44411340 | solution.py:86
  9.7 5.4 %fusion.60 = (f32[4096]{0:T(1024)S(1)}, f32[4096,320]{0,1:T(8,128)S(1)}) fusion(f32[320]{0:T(512)S(1)} %dynamic-slice_reduce_fusion.2, f32[4,320]{1,0:T(4,128)} %get-tuple-element.315, f32[4,4,4096]{2,1,0:T(4,128)} %get-tuple-element.314, s32[]{:T(128)} %get-tuple-element.300), kind=kOutput, calls=%fused_computation.72.clone.1 | convolution fusion | flops 65531904 | bytes 5332736 | tf_op jit(solution)/shard_map/while/body/eval_jaxpr/dot_general | solution.py:75
  15.1 0.6 multiply_reduce_fusion.2
  15.8 1.6 fusion.61
  17.4 13.1 %fusion.62 = bf16[320,4096]{1,0:T(8,128)(2,1)S(1)} fusion(bf16[320,320]{1,0:T(8,128)(2,1)S(1)} %copy-done.8, f32[4096,320]{0,1:T(8,128)S(1)} %fusion.61, f32[4096,320]{0,1:T(8,128)S(1)} %get-tuple-element.283, f32[4096]{0:T(1024)S(1)} %add_rsqrt_fusion.2, f32[4096]{0:T(1024)S(1)} %broadcast_multiply_fusion.2), kind=kOutput, calls=%fused_computation.5.clone.1 | convolution fusion | flops 929300480 | bytes 13344768 | tf_op jit(solution)/shard_map/while/body/eval_jaxpr/cf,cp->fp/dot_general | solution.py:80
  30.5 1.1 fusion.63
  31.7 2.8 fusion.64
  34.6 5.3 %fusion.60 = (f32[4096]{0:T(1024)S(1)}, f32[4096,320]{0,1:T(8,128)S(1)}) fusion(f32[320]{0:T(512)S(1)} %dynamic-slice_reduce_fusion.2, f32[4,320]{1,0:T(4,128)} %get-tuple-element.315, f32[4,4,4096]{2,1,0:T(4,128)} %get-tuple-element.314, s32[]{:T(128)} %get-tuple-element.300), kind=kOutput, calls=%fused_computation.72.clone.1 | convolution fusion | flops 65531904 | bytes 5332736 | tf_op jit(solution)/shard_map/while/body/eval_jaxpr/dot_general | solution.py:75
  39.9 0.6 multiply_reduce_fusion.2
  40.6 1.6 fusion.61
  42.2 13.1 %fusion.62 = bf16[320,4096]{1,0:T(8,128)(2,1)S(1)} fusion(bf16[320,320]{1,0:T(8,128)(2,1)S(1)} %copy-done.8, f32[4096,320]{0,1:T(8,128)S(1)} %fusion.61, f32[4096,320]{0,1:T(8,128)S(1)} %get-tuple-element.283, f32[4096]{0:T(1024)S(1)} %add_rsqrt_fusion.2, f32[4096]{0:T(1024)S(1)} %broadcast_multiply_fusion.2), kind=kOutput, calls=%fused_computation.5.clone.1 | convolution fusion | flops 929300480 | bytes 13344768 | tf_op jit(solution)/shard_map/while/body/eval_jaxpr/cf,cp->fp/dot_general | solution.py:80
  55.3 1.1 fusion.63
  56.5 2.8 fusion.64
  59.4 5.3 %fusion.60 = (f32[4096]{0:T(1024)S(1)}, f32[4096,320]{0,1:T(8,128)S(1)}) fusion(f32[320]{0:T(512)S(1)} %dynamic-slice_reduce_fusion.2, f32[4,320]{1,0:T(4,128)} %get-tuple-element.315, f32[4,4,4096]{2,1,0:T(4,128)} %get-tuple-element.314, s32[]{:T(128)} %get-tuple-element.300), kind=kOutput, calls=%fused_computation.72.clone.1 | convolution fusion | flops 65531904 | bytes 5332736 | tf_op jit(solution)/shard_map/while/body/eval_jaxpr/dot_general | solution.py:75
  65.4 1.6 fusion.61
  67.0 13.1 %fusion.62 = bf16[320,4096]{1,0:T(8,128)(2,1)S(1)} fusion(bf16[320,320]{1,0:T(8,128)(2,1)S(1)} %copy-done.8, f32[4096,320]{0,1:T(8,128)S(1)} %fusion.61, f32[4096,320]{0,1:T(8,128)S(1)} %get-tuple-element.283, f32[4096]{0:T(1024)S(1)} %add_rsqrt_fusion.2, f32[4096]{0:T(1024)S(1)} %broadcast_multiply_fusion.2), kind=kOutput, calls=%fused_computation.5.clone.1 | convolution fusion | flops 929300480 | bytes 13344768 | tf_op jit(solution)/shard_map/while/body/eval_jaxpr/cf,cp->fp/dot_general | solution.py:80
  80.1 1.1 fusion.63
  81.3 2.8 fusion.64
  84.2 5.3 %fusion.60 = (f32[4096]{0:T(1024)S(1)}, f32[4096,320]{0,1:T(8,128)S(1)}) fusion(f32[320]{0:T(512)S(1)} %dynamic-slice_reduce_fusion.2, f32[4,320]{1,0:T(4,128)} %get-tuple-element.315, f32[4,4,4096]{2,1,0:T(4,128)} %get-tuple-element.314, s32[]{:T(128)} %get-tuple-element.300), kind=kOutput, calls=%fused_computation.72.clone.1 | convolution fusion | flops 65531904 | bytes 5332736 | tf_op jit(solution)/shard_map/while/body/eval_jaxpr/dot_general | solution.py:75
  90.2 1.6 fusion.61
  91.8 13.1 %fusion.62 = bf16[320,4096]{1,0:T(8,128)(2,1)S(1)} fusion(bf16[320,320]{1,0:T(8,128)(2,1)S(1)} %copy-done.8, f32[4096,320]{0,1:T(8,128)S(1)} %fusion.61, f32[4096,320]{0,1:T(8,128)S(1)} %get-tuple-element.283, f32[4096]{0:T(1024)S(1)} %add_rsqrt_fusion.2, f32[4096]{0:T(1024)S(1)} %broadcast_multiply_fusion.2), kind=kOutput, calls=%fused_computation.5.clone.1 | convolution fusion | flops 929300480 | bytes 13344768 | tf_op jit(solution)/shard_map/while/body/eval_jaxpr/cf,cp->fp/dot_general | solution.py:80
  105.0 1.1 fusion.63
  106.1 2.8 fusion.64
  109.0 0.7 copy-done.3
  110.5 18.7 %all-gather.5.cloned.1.call-done = f32[16,4,4096]{2,1,0:T(4,128)} async-done(((f32[4,4,4096]{2,1,0:T(4,128)}), f32[16,4,4096]{2,1,0:T(4,128)}) %all-gather.5.cloned.1.call-update) | async-done | bytes 1048592 | tf_op jit(solution)/shard_map/all_gather | solution.py:87
  129.3 1.5 reduce_sum.51
  130.8 1.9 fusion.26
  132.7 49.2 %all-gather.7.cloned.1.call-done = f32[32,1,4,4096]{3,2,1,0:T(4,128)} async-done(((f32[4,1,4,4096]{3,2,1,0:T(4,128)}), f32[32,1,4,4096]{3,2,1,0:T(4,128)}) %all-gather.7.cloned.1.call-update) | async-done | bytes 2097168 | tf_op jit(solution)/shard_map/all_gather | solution.py:12
  181.9 10.1 %while.27 = (s32[]{:T(128)}, f32[4,4,4096]{2,1,0:T(4,128)S(1)}, s32[]{:T(128)}, f32[8,4,4,4096]{3,2,1,0:T(4,128)}, s32[]{:T(128)}, /*index=5*/s32[]{:T(128)}) while((s32[]{:T(128)}, f32[4,4,4096]{2,1,0:T(4,128)S(1)}, s32[]{:T(128)}, f32[8,4,4,4096]{3,2,1,0:T(4,128)}, s32[]{:T(128)}, /*index=5*/s32[]{:T(128)}) %tuple.75), condition=%wide.region_10.11_spmd.clone, body=%wide.region_9.10_spmd.clone.sunk | while | flops 196612 | bytes 786525 | solution.py:20
  181.9 1.2 add_select_fusion.2
  183.2 1.2 add_select_fusion.2
  184.4 1.2 add_select_fusion.2
  185.7 1.2 add_select_fusion.2
  186.9 1.2 add_select_fusion.2
  188.2 1.2 add_select_fusion.2
  189.5 1.2 add_select_fusion.2
  190.7 1.2 add_select_fusion.2
  192.0 1.8 broadcast_select_fusion
  193.8 1.3 collective-permute-start
  195.1 6.9 %collective-permute-done = f32[4,1,4,4096]{3,2,1,0:T(4,128)S(1)} collective-permute-done((f32[4,1,4,4096]{3,2,1,0:T(4,128)S(1)}, f32[4,1,4,4096]{3,2,1,0:T(4,128)S(1)}, u32[]{:S(2)}, u32[]{:S(2)}) %collective-permute-start) | collective-permute-done | bytes 262176 | tf_op jit(solution)/shard_map/ppermute | solution.py:31
  202.2 1.3 collective-permute-start.1
  203.5 7.1 %collective-permute-done.1 = f32[4,1,4,4096]{3,2,1,0:T(4,128)S(1)} collective-permute-done((f32[4,1,4,4096]{3,2,1,0:T(4,128)S(1)}, f32[4,1,4,4096]{3,2,1,0:T(4,128)S(1)}, u32[]{:S(2)}, u32[]{:S(2)}) %collective-permute-start.1) | collective-permute-done | bytes 262176 | tf_op jit(solution)/shard_map/ppermute | solution.py:31
  210.7 1.3 collective-permute-start.2
  212.0 0.6 dynamic-slice_bitcast_fusion
  212.7 69.9 %all-reduce.3.cloned.1.call-done = f32[4,1,4,4096]{3,2,1,0:T(4,128)} async-done(((f32[4,1,4,4096]{3,2,1,0:T(4,128)}), f32[4,1,4,4096]{3,2,1,0:T(4,128)}) %all-reduce.3.cloned.1.call-update) | async-done | bytes 262160 | tf_op jit(solution)/shard_map/psum | solution.py:25
  282.5 1.8 select_select_fusion
  (75 shorter events, 2.9 us)
Async XLA Ops:
  7.2 1.5 copy-start
  7.2 122.1 %all-gather.5.cloned.1.call-start = ((), (), s32[]{:S(2)}) async-start(), calls=%async_computation.1 | async-start | bytes 1310720 | tf_op jit(solution)/shard_map/all_gather | solution.py:87
  9.6 100.7 %copy-start.6 = (s32[4]{0:T(128)S(1)}, s32[4]{0:T(128)}, u32[]{:S(2)}) copy-start(s32[4]{0:T(128)} %get-tuple-element.187) | copy-start | bytes 52
  9.7 121.1 %copy-start.4 = (f32[4,1,4,4096]{3,2,1,0:T(4,128)S(1)}, f32[4,1,4,4096]{3,2,1,0:T(4,128)}, u32[]{:S(2)}) copy-start(f32[4,1,4,4096]{3,2,1,0:T(4,128)} %param.14) | copy-start | bytes 786436
  9.7 6.0 %copy-start.1 = (bf16[320,320]{1,0:T(8,128)(2,1)S(1)}, bf16[320,320]{1,0:T(8,128)(2,1)}, u32[]{:S(2)}) copy-start(bf16[320,320]{1,0:T(8,128)(2,1)} %get-tuple-element.317) | copy-start | bytes 614404 | tf_op jit(solution)/shard_map/while
  15.8 1.6 copy-start.8
  17.4 14.3 %copy-start.5 = (f32[320,4]{0,1:T(4,128)S(1)}, f32[320,4]{0,1:T(4,128)}, u32[]{:S(2)}) copy-start(f32[320,4]{0,1:T(4,128)} %get-tuple-element.320) | copy-start | bytes 15364 | tf_op jit(solution)/shard_map/while
  34.6 6.0 %copy-start.1 = (bf16[320,320]{1,0:T(8,128)(2,1)S(1)}, bf16[320,320]{1,0:T(8,128)(2,1)}, u32[]{:S(2)}) copy-start(bf16[320,320]{1,0:T(8,128)(2,1)} %get-tuple-element.317) | copy-start | bytes 614404 | tf_op jit(solution)/shard_map/while
  40.6 1.6 copy-start.8
  42.2 14.3 %copy-start.5 = (f32[320,4]{0,1:T(4,128)S(1)}, f32[320,4]{0,1:T(4,128)}, u32[]{:S(2)}) copy-start(f32[320,4]{0,1:T(4,128)} %get-tuple-element.320) | copy-start | bytes 15364 | tf_op jit(solution)/shard_map/while
  59.3 6.0 %copy-start.1 = (bf16[320,320]{1,0:T(8,128)(2,1)S(1)}, bf16[320,320]{1,0:T(8,128)(2,1)}, u32[]{:S(2)}) copy-start(bf16[320,320]{1,0:T(8,128)(2,1)} %get-tuple-element.317) | copy-start | bytes 614404 | tf_op jit(solution)/shard_map/while
  65.4 1.6 copy-start.8
  67.0 14.3 %copy-start.5 = (f32[320,4]{0,1:T(4,128)S(1)}, f32[320,4]{0,1:T(4,128)}, u32[]{:S(2)}) copy-start(f32[320,4]{0,1:T(4,128)} %get-tuple-element.320) | copy-start | bytes 15364 | tf_op jit(solution)/shard_map/while
  84.2 6.0 %copy-start.1 = (bf16[320,320]{1,0:T(8,128)(2,1)S(1)}, bf16[320,320]{1,0:T(8,128)(2,1)}, u32[]{:S(2)}) copy-start(bf16[320,320]{1,0:T(8,128)(2,1)} %get-tuple-element.317) | copy-start | bytes 614404 | tf_op jit(solution)/shard_map/while
  90.2 1.6 copy-start.8
  91.8 14.3 %copy-start.5 = (f32[320,4]{0,1:T(4,128)S(1)}, f32[320,4]{0,1:T(4,128)}, u32[]{:S(2)}) copy-start(f32[320,4]{0,1:T(4,128)} %get-tuple-element.320) | copy-start | bytes 15364 | tf_op jit(solution)/shard_map/while
  108.9 0.7 copy-start.3
  109.0 83.0 %copy-start.2 = (f32[4,4,4096]{2,1,0:T(4,128)S(1)}, f32[4,4,4096]{2,1,0:T(4,128)}, u32[]{:S(2)}) copy-start(f32[4,4,4096]{2,1,0:T(4,128)} %get-tuple-element.343) | copy-start | bytes 786436
  109.0 86.1 %copy-start.7 = (s32[4]{0:T(128)S(1)}, s32[4]{0:T(128)}, u32[]{:S(2)}) copy-start(s32[4]{0:T(128)} %param.16) | copy-start | bytes 52
  109.7 72.2 %all-gather.7.cloned.1.call-start = ((), (), s32[]{:S(2)}) async-start(), calls=%async_computation.2 | async-start | bytes 2359296 | tf_op jit(solution)/shard_map/all_gather | solution.py:12
  132.7 149.9 %all-reduce.3.cloned.1.call-start = ((), (), s32[]{:S(2)}) async-start(), calls=%async_computation | async-start | bytes 524288 | tf_op jit(solution)/shard_map/psum | solution.py:25
  193.8 8.3 %collective-permute-start = (f32[4,1,4,4096]{3,2,1,0:T(4,128)S(1)}, f32[4,1,4,4096]{3,2,1,0:T(4,128)S(1)}, u32[]{:S(2)}, u32[]{:S(2)}) collective-permute-start(f32[4,1,4,4096]{3,2,1,0:T(4,128)S(1)} %get-tuple-element.183), channel_id=1, source_target_pairs={{4,0},{8,4},{12,8},{16,12},{20,16},{24,20},{28,24},{5,1},{9,5},{13... | collective-permute-start | bytes 786440 | tf_op jit(solution)/shard_map/ppermute | solution.py:31
  202.2 8.4 %collective-permute-start.1 = (f32[4,1,4,4096]{3,2,1,0:T(4,128)S(1)}, f32[4,1,4,4096]{3,2,1,0:T(4,128)S(1)}, u32[]{:S(2)}, u32[]{:S(2)}) collective-permute-start(f32[4,1,4,4096]{3,2,1,0:T(4,128)S(1)} %broadcast_select_fusion.1), channel_id=1, source_target_pairs={{8,0},{12,4},{16,8},{20,12},{24,16},{28,20},{9,1},{13,5},{17,9},{2... | collective-permute-start | bytes 786440 | tf_op jit(solution)/shard_map/ppermute | solution.py:31
  210.7 71.8 %collective-permute-start.2 = (f32[4,1,4,4096]{3,2,1,0:T(4,128)S(1)}, f32[4,1,4,4096]{3,2,1,0:T(4,128)S(1)}, u32[]{:S(2)}, u32[]{:S(2)}) collective-permute-start(f32[4,1,4,4096]{3,2,1,0:T(4,128)S(1)} %broadcast_select_fusion.2), channel_id=1, source_target_pairs={{16,0},{20,4},{24,8},{28,12},{17,1},{21,5},{25,9},{29,13},{18,2},{... | collective-permute-start | bytes 786440 | tf_op jit(solution)/shard_map/ppermute | solution.py:31
Sparse Core Ops, SparseCore 0:
  109.8 19.4 all-gather.4
  132.8 49.0 all-gather.6
  203.6 78.8 all-reduce.2
